TPU v7x, 32 devices: a whole 2x2x4 slice. The times are simulated.
32 devices in a mesh: dp: 8 (over z, y), head: 4 (over x, core).
Axes of the slice: x: 2, y: 2, z: 4, core: 2. Of those that a mesh axis runs over, the one named last changes fastest.
Arguments:
- tokens: bfloat16 [32768, 768], P(('dp', 'head')), may hold values from -6 to 6
- seq_lengths: int32 [64, 32], P('dp'), may hold values from 0 to 512, as said below
- qkv_weight: bfloat16 [2, 3, 768, 768], P(None, None, None, 'head'), may hold values from -0.21875 to 0.21875
- qv_bias: float32 [2, 2, 768], P(None, None, 'head'), may hold values from -3 to 3
- out_weight: bfloat16 [2, 768, 768], replicated, may hold values from -0.875 to 0.875
- out_bias: float32 [2, 768], replicated, may hold values from -3 to 3
- norm1_gain: float32 [2, 768], replicated, may hold values from 0.25 to 1.75
- norm1_shift: float32 [2, 768], replicated, may hold values from -3 to 3
- up_weight: bfloat16 [2, 768, 3072], replicated, may hold values from -0.21875 to 0.21875
- up_bias: float32 [2, 3072], replicated, may hold values from -3 to 3
- down_weight: bfloat16 [2, 3072, 768], replicated, may hold values from -0.109375 to 0.109375
- down_bias: float32 [2, 768], replicated, may hold values from -3 to 3
- norm2_gain: float32 [2, 768], replicated, may hold values from 0.25 to 1.75
- norm2_shift: float32 [2, 768], replicated, may hold values from -3 to 3
- out_grad: bfloat16 [32768, 768], P(('dp', 'head')), may hold values from -6 to 6
Outputs:
- out_state: bfloat16 [32768, 768], P(('dp', 'head'))
- input_grad: bfloat16 [32768, 768], P(('dp', 'head'))
- qkv_weight_grad: float32 [2, 3, 768, 768], P(None, None, 'dp', 'head')
- qv_bias_grad: float32 [2, 2, 768], replicated
- out_weight_grad: float32 [2, 768, 768], P(None, 'dp', 'head')
- out_bias_grad: float32 [2, 768], replicated
- norm1_gain_grad: float32 [2, 768], replicated
- norm1_shift_grad: float32 [2, 768], replicated
- up_weight_grad: float32 [2, 768, 3072], P(None, 'dp', 'head')
- up_bias_grad: float32 [2, 3072], replicated
- down_weight_grad: float32 [2, 3072, 768], P(None, 'head', 'dp')
- down_bias_grad: float32 [2, 768], replicated
- norm2_gain_grad: float32 [2, 768], replicated
- norm2_shift_grad: float32 [2, 768], replicated
Inputs may be any that keep to these rules, and one draw needn't show every extreme that they name: `seq_lengths`: each slot's row sums to 512; nonzero entries come first and zero entries mark no sequence; some slot holds a single sequence of 512 rows.
All inputs are finite; a program needn't handle non-finite values.
Results may differ from a plain program's by a relative error of at most 0.025.
Values may be sent and summed in bfloat16 or wider, within the bound.
No kernel may reach another device: no remote copies, remote signals or barrier semaphores. Data moves between devices by JAX's collectives and lax.ppermute only.
A program may use at most 256 MiB of HBM per device.

v0:
```python
import jax
import jax.numpy as jnp
from jax import lax
from jax.sharding import PartitionSpec as P

HD = 64
EPSILON = 1e-06


def norm_rows(values, gain, shift):
    centre = jnp.mean(values, axis=-1, keepdims=True)
    centred = values - centre
    spread = jnp.mean(centred * centred, axis=-1, keepdims=True)
    return centred * lax.rsqrt(spread + EPSILON) * gain + shift


def exact_gelu(values):
    return jax.nn.gelu(values, approximate=False)


def segment_ids(lengths, slot_rows):
    boundary = jnp.cumsum(lengths, axis=1)
    position = jnp.arange(slot_rows, dtype=jnp.int32)
    return jnp.sum((position[None, :, None] >= boundary[:, None, :]).astype(jnp.int32), axis=2)


def slot_scores(queries, keys_in, segments):
    scaling = queries.shape[-1] ** (-0.5)
    scores = (
        jnp.einsum("qhd,khd->hqk", queries, keys_in, preferred_element_type=jnp.float32) * scaling
    )
    inside = (segments[:, None] == segments[None, :])[None]
    return (scores, inside)


def slot_forward(packed):
    queries, keys_in, values_in, segments = packed
    scores, inside = slot_scores(queries, keys_in, segments)
    scores = jnp.where(inside, scores, -1e30)
    peak_score = jnp.max(scores, axis=-1, keepdims=True)
    weights = jnp.exp(scores - peak_score)
    denominator = jnp.sum(weights, axis=-1, keepdims=True)
    probability = (weights / denominator).astype(jnp.bfloat16)
    context = jnp.einsum("hqk,khd->qhd", probability, values_in, preferred_element_type=jnp.float32)
    return (context.astype(jnp.bfloat16), (peak_score + jnp.log(denominator))[..., 0])


def slot_backward(packed):
    queries, keys_in, values_in, grad_context, log_total, segments = packed
    scaling = queries.shape[-1] ** (-0.5)
    scores, inside = slot_scores(queries, keys_in, segments)
    probability = jnp.where(inside, jnp.exp(scores - log_total[..., None]), 0.0)
    grad_prob = jnp.einsum(
        "qhd,khd->hqk", grad_context, values_in, preferred_element_type=jnp.float32
    )
    shares = jnp.sum(probability * grad_prob, axis=-1, keepdims=True)
    grad_score = (probability * (grad_prob - shares)).astype(jnp.bfloat16)
    grad_query = (
        jnp.einsum("hqk,khd->qhd", grad_score, keys_in, preferred_element_type=jnp.float32)
        * scaling
    )
    grad_key = (
        jnp.einsum("hqk,qhd->khd", grad_score, queries, preferred_element_type=jnp.float32)
        * scaling
    )
    grad_value = jnp.einsum(
        "hqk,qhd->khd",
        probability.astype(jnp.bfloat16),
        grad_context,
        preferred_element_type=jnp.float32,
    )
    return (
        grad_query.astype(jnp.bfloat16),
        grad_key.astype(jnp.bfloat16),
        grad_value.astype(jnp.bfloat16),
    )


def on_device(
    tokens,
    seq_lengths,
    qkv_weight,
    qv_bias,
    out_weight,
    out_bias,
    norm1_gain,
    norm1_shift,
    up_weight,
    up_bias,
    down_weight,
    down_bias,
    norm2_gain,
    norm2_shift,
    out_grad,
):
    heads_count = lax.axis_size("head")
    head_index = lax.axis_index("head")
    local_rows, model_width = tokens.shape
    group_rows = local_rows * heads_count
    slots_here = seq_lengths.shape[0]
    slot_rows = group_rows // slots_here
    segments = segment_ids(seq_lengths, slot_rows)
    head_width = qkv_weight.shape[-1]
    local_heads = head_width // HD
    layers = qkv_weight.shape[0]
    qkv_shape = (slots_here, slot_rows, 3, local_heads, HD)
    hidden_state = tokens.astype(jnp.float32)
    kept_values = []
    for layer_index in range(layers):
        gathered = lax.all_gather(hidden_state.astype(jnp.bfloat16), "head", axis=0, tiled=True)
        projected = jnp.einsum(
            "rd,cde->rce", gathered, qkv_weight[layer_index], preferred_element_type=jnp.float32
        )
        bias_rows = jnp.stack(
            [
                qv_bias[layer_index, 0],
                jnp.zeros_like(qv_bias[layer_index, 0]),
                qv_bias[layer_index, 1],
            ]
        )
        projected = (projected + bias_rows[None]).astype(jnp.bfloat16)
        shaped = projected.reshape(qkv_shape)
        context, log_total = lax.map(
            slot_forward, (shaped[:, :, 0], shaped[:, :, 1], shaped[:, :, 2], segments)
        )
        context = context.reshape(group_rows, head_width)
        token_context = lax.all_to_all(context, "head", split_axis=0, concat_axis=1, tiled=True)
        attended = (
            jnp.dot(token_context, out_weight[layer_index], preferred_element_type=jnp.float32)
            + out_bias[layer_index]
        )
        first_sum = hidden_state + attended
        normed = norm_rows(first_sum, norm1_gain[layer_index], norm1_shift[layer_index])
        normed_low = normed.astype(jnp.bfloat16)
        ffn_rows = normed_low
        up_part = up_weight[layer_index]
        up_shift = up_bias[layer_index]
        down_part = down_weight[layer_index]
        before_gelu = jnp.dot(ffn_rows, up_part, preferred_element_type=jnp.float32) + up_shift
        activated = exact_gelu(before_gelu).astype(jnp.bfloat16)
        branch = jnp.dot(activated, down_part, preferred_element_type=jnp.float32)
        second_sum = normed + branch + down_bias[layer_index]
        hidden_state = norm_rows(second_sum, norm2_gain[layer_index], norm2_shift[layer_index])
        kept_values.append(
            (
                gathered,
                projected,
                log_total,
                token_context,
                first_sum,
                ffn_rows,
                up_part,
                down_part,
                before_gelu,
                activated,
                second_sum,
            )
        )
    out_state = hidden_state.astype(jnp.bfloat16)
    grad_state = out_grad.astype(jnp.float32)
    ffn_list, proj_list, attn_list, small_list, shift_list = ([], [], [], [], [])
    for layer_index in reversed(range(layers)):
        (
            gathered,
            projected,
            log_total,
            token_context,
            first_sum,
            ffn_rows,
            up_part,
            down_part,
            before_gelu,
            activated,
            second_sum,
        ) = kept_values[layer_index]
        pull_second = jax.vjp(
            norm_rows, second_sum, norm2_gain[layer_index], norm2_shift[layer_index]
        )[1]
        grad_second, grad_gain2, grad_shift2 = pull_second(grad_state)
        grad_branch = grad_second.astype(jnp.bfloat16)
        grad_down_shift = jnp.sum(grad_branch.astype(jnp.float32), axis=0)
        grad_down = jnp.einsum(
            "rd,rf->df", grad_branch, activated, preferred_element_type=jnp.float32
        )
        grad_act = jnp.einsum(
            "rd,fd->rf", grad_branch, down_part, preferred_element_type=jnp.float32
        )
        pull_gelu = jax.vjp(exact_gelu, before_gelu)[1]
        grad_pre = pull_gelu(grad_act)[0].astype(jnp.bfloat16)
        grad_up_shift = jnp.sum(grad_pre.astype(jnp.float32), axis=0)
        grad_up = jnp.einsum("rd,rf->df", ffn_rows, grad_pre, preferred_element_type=jnp.float32)
        grad_normed_low = jnp.einsum(
            "rf,df->rd", grad_pre, up_part, preferred_element_type=jnp.float32
        )
        grad_normed = grad_second + grad_normed_low
        pull_first = jax.vjp(
            norm_rows, first_sum, norm1_gain[layer_index], norm1_shift[layer_index]
        )[1]
        grad_first, grad_gain1, grad_shift1 = pull_first(grad_normed)
        grad_attended = grad_first.astype(jnp.bfloat16)
        grad_out_shift = jnp.sum(grad_attended.astype(jnp.float32), axis=0)
        grad_out = jnp.einsum(
            "rd,re->de", token_context, grad_attended, preferred_element_type=jnp.float32
        )
        grad_mixed = jnp.einsum(
            "re,de->rd", grad_attended, out_weight[layer_index], preferred_element_type=jnp.float32
        ).astype(jnp.bfloat16)
        grad_context = lax.all_to_all(grad_mixed, "head", split_axis=1, concat_axis=0, tiled=True)
        shaped = projected.reshape(qkv_shape)
        grad_query, grad_key, grad_value = lax.map(
            slot_backward,
            (
                shaped[:, :, 0],
                shaped[:, :, 1],
                shaped[:, :, 2],
                grad_context.reshape(slots_here, slot_rows, local_heads, HD),
                log_total,
                segments,
            ),
        )
        grad_proj = jnp.stack([grad_query, grad_key, grad_value], axis=2).reshape(
            group_rows, 3, head_width
        )
        grad_qkv = jnp.einsum(
            "rd,rce->cde", gathered, grad_proj, preferred_element_type=jnp.float32
        )
        bias_local = jnp.sum(grad_proj.astype(jnp.float32), axis=0)
        qv_local = jnp.stack([bias_local[0], bias_local[2]])
        qv_full = lax.dynamic_update_slice_in_dim(
            jnp.zeros((2, model_width), jnp.float32), qv_local, head_index * head_width, 1
        )
        layer_weights = qkv_weight[layer_index]
        grad_state = grad_first + lax.psum_scatter(
            jnp.einsum(
                "rce,cde->rd", grad_proj, layer_weights, preferred_element_type=jnp.float32
            ).astype(jnp.bfloat16),
            "head",
            scatter_dimension=0,
            tiled=True,
        ).astype(jnp.float32)
        ffn_list.append(jnp.stack([grad_up, grad_down]))
        proj_list.append(grad_out)
        attn_list.append(grad_qkv)
        small_list.append(
            jnp.concatenate(
                [
                    qv_full,
                    jnp.stack(
                        [
                            grad_out_shift,
                            grad_gain1,
                            grad_shift1,
                            grad_down_shift,
                            grad_gain2,
                            grad_shift2,
                        ]
                    ),
                ],
                axis=0,
            )
        )
        shift_list.append(grad_up_shift)
    input_grad = grad_state.astype(jnp.bfloat16)
    ffn_stack = jnp.stack(ffn_list[::-1])
    proj_stack = jnp.stack(proj_list[::-1])
    attn_stack = jnp.stack(attn_list[::-1])
    small_stack = jnp.stack(small_list[::-1])
    shift_stack = jnp.stack(shift_list[::-1])
    ffn_data, proj_data, attn_data = (
        lax.psum_scatter(
            ffn_stack.astype(jnp.bfloat16), "dp", scatter_dimension=2, tiled=True
        ).astype(jnp.float32),
        lax.psum_scatter(
            proj_stack.astype(jnp.bfloat16), "dp", scatter_dimension=1, tiled=True
        ).astype(jnp.float32),
        lax.psum_scatter(
            attn_stack.astype(jnp.bfloat16), "dp", scatter_dimension=2, tiled=True
        ).astype(jnp.float32),
    )
    ffn_head, proj_head = (
        lax.psum_scatter(
            ffn_data.astype(jnp.bfloat16), "head", scatter_dimension=3, tiled=True
        ).astype(jnp.float32),
        lax.psum_scatter(
            proj_data.astype(jnp.bfloat16), "head", scatter_dimension=2, tiled=True
        ).astype(jnp.float32),
    )
    small_sum, shift_sum = lax.psum((small_stack, shift_stack), ("dp", "head"))
    down_weight_grad = jnp.transpose(ffn_head[:, 1], (0, 2, 1))
    return (
        out_state,
        input_grad,
        attn_data,
        small_sum[:, 0:2],
        proj_head,
        small_sum[:, 2],
        small_sum[:, 3],
        small_sum[:, 4],
        ffn_head[:, 0],
        shift_sum,
        down_weight_grad,
        small_sum[:, 5],
        small_sum[:, 6],
        small_sum[:, 7],
    )


def solution(mesh):
    in_specs = (
        P(("dp", "head"), None),
        P("dp", None),
        P(None, None, None, "head"),
        P(None, None, "head"),
        P(),
        P(),
        P(),
        P(),
        P(),
        P(),
        P(),
        P(),
        P(),
        P(),
        P(("dp", "head"), None),
    )
    out_specs = (
        P(("dp", "head"), None),
        P(("dp", "head"), None),
        P(None, None, "dp", "head"),
        P(),
        P(None, "dp", "head"),
        P(),
        P(),
        P(),
        P(None, "dp", "head"),
        P(),
        P(None, "head", "dp"),
        P(),
        P(),
        P(),
    )
    return jax.shard_map(
        on_device, mesh=mesh, in_specs=in_specs, out_specs=out_specs, check_vma=False
    )
```

profile of v0, /device:TPU:0, one launch (start us, length us, event | category | flops | bytes accessed | tf_op | source)
XLA Modules:
  0.0 1406.1 jit_solution(3311266776964060774)
XLA Ops:
  12.9 45.8 %all-gather.3.cloned.1.call-done = bf16[4096,768]{1,0:T(8,128)(2,1)} async-done(((bf16[1024,768]{1,0:T(8,128)(2,1)}), bf16[4096,768]{1,0:T(8,128)(2,1)}) %all-gather.3.cloned.1.call-update) | async-done | bytes 6291472 | tf_op jit(solution)/shard_map/all_gather | solution.py:110
  73.9 35.4 %while.52 = (s32[]{:T(128)}, bf16[8,512,3,64]{1,3,2,0:T(8,128)(2,1)}, f32[8,3,512]{2,1,0:T(4,128)S(1)}, bf16[8,512,3,64]{1,3,2,0:T(8,128)(2,1)}, s32[8,512]{1,0:...) while((s32[]{:T(128)}, ...), condition=%wide.region_5.6_spmd, body=%wide.region_2.5_spmd.sunk | while | flops 211122688 | bytes 11335773 | solution.py:123
  113.8 13.7 all_to_all.52
  139.1 15.2 %all-to-all-done = bf16[4,1024,192]{1,2,0:T(8,128)(2,1)S(1)} async-done(((bf16[4,1024,192]{1,2,0:T(8,128)(2,1)}), bf16[4,1024,192]{1,2,0:T(8,128)(2,1)S(1)}, u32[]{:S(2)}, u32[]{:S(2)}) %all-to-all-start) | async-done | bytes 1572896 | tf_op jit(solution)/shard_map/all_to_all | solution.py:127
  158.9 38.8 %multiply_convert_fusion.3 = (bf16[1024,3072]{1,0:T(8,128)(2,1)}, f32[1024,3072]{1,0:T(8,128)}, f32[1024,3072]{1,0:T(8,128)}) fusion(f32[3072]{0:T(1024)S(1)} %bitcast.494, bf16[2,768,3072]{2,1,0:T(8,128)(2,1)} %param.31, f32[1024,768]{0,1:T(8,128)S(1)} %get-tuple-element.478, f32[768]{0:T(1024)S(1)} %get-tuple-element.347, ...), kind=kOutput, calls=%fused_computation.148 | convolution fusion | flops 5043388416 | bytes 39348224 | tf_op jit(solution)/shard_map/dot_general | solution.py:139
  208.6 46.5 %all-gather.5.cloned.1.call-done = bf16[4096,768]{0,1:T(8,128)(2,1)} async-done(((bf16[1024,768]{0,1:T(8,128)(2,1)}), bf16[4096,768]{0,1:T(8,128)(2,1)}) %all-gather.5.cloned.1.call-update) | async-done | bytes 6291472 | tf_op jit(solution)/shard_map/all_gather | solution.py:110
  273.1 43.5 %while.53 = (s32[]{:T(128)}, bf16[8,512,3,64]{1,3,2,0:T(8,128)(2,1)}, f32[8,3,512]{2,1,0:T(4,128)S(1)}, bf16[8,512,3,64]{1,3,2,0:T(8,128)(2,1)}, s32[8,512]{1,0:...) while((s32[]{:T(128)}, ...), condition=%wide.region_13.14_spmd, body=%wide.region_10.13_spmd.sunk | while | flops 211122688 | bytes 11335773 | solution.py:123
  334.3 17.5 %all-to-all-done.1 = bf16[4,1024,192]{1,2,0:T(8,128)(2,1)} async-done(((bf16[4,1024,192]{1,2,0:T(8,128)(2,1)}), bf16[4,1024,192]{1,2,0:T(8,128)(2,1)}, u32[]{:S(2)}, u32[]{:S(2)}) %all-to-all-start.1) | async-done | bytes 1572896 | tf_op jit(solution)/shard_map/all_to_all | solution.py:127
  356.5 38.4 %multiply_convert_fusion.2 = (bf16[1024,3072]{1,0:T(8,128)(2,1)}, f32[1024,3072]{1,0:T(8,128)}, f32[1024,3072]{1,0:T(8,128)}) fusion(f32[3072]{0:T(1024)S(1)} %bitcast.497, bf16[2,768,3072]{2,1,0:T(8,128)(2,1)} %param.31, f32[1024,768]{0,1:T(8,128)S(1)} %get-tuple-element.483, f32[768]{0:T(1024)S(1)} %copy-done.73, f32[768]{0:T(1024)S(1)} %copy-done.52, ...), kind=kOutput, calls=%fused_computation.135 | convolution fusion | flops 5043388416 | bytes 39348224 | tf_op jit(solution)/shard_map/dot_general | solution.py:139
  411.1 18.2 %convert_reduce_fusion = (f32[3072]{0:T(1024)}, bf16[1024,3072]{1,0:T(8,128)(2,1)}) fusion(f32[1024,3072]{1,0:T(8,128)} %get-tuple-element.435, bf16[1024,768]{0,1:T(8,128)(2,1)S(1)} %get-tuple-element.425, bf16[2,3072,768]{2,1,0:T(8,128)(2,1)} %param.33, f32[1024,3072]{1,0:T(8,128)} %get-tuple-element.484, f32[3072]{0:T(1024)S(1)} %bitcast.498), kind=kOutput, calls=%fused_computation.131 | convolution fusion | flops 4885312512 | bytes 37773312 | tf_op jit(solution)/shard_map/rd,fd->rf/dot_general | solution.py:185
  429.4 11.7 multiply_reduce_fusion.2
  451.5 20.0 %all-to-all-done.2 = bf16[1024,4,192]{0,2,1:T(8,128)(2,1)S(1)} async-done(((bf16[1024,4,192]{0,2,1:T(8,128)(2,1)}), bf16[1024,4,192]{0,2,1:T(8,128)(2,1)S(1)}, u32[]{:S(2)}, u32[]{:S(2)}) %all-to-all-start.2) | async-done | bytes 1572896 | tf_op jit(solution)/shard_map/all_to_all | solution.py:208
  479.6 88.1 %while.54 = (s32[]{:T(128)}, bf16[8,512,3,64]{1,3,2,0:T(8,128)(2,1)S(1)}, bf16[8,512,3,64]{1,3,2,0:T(8,128)(2,1)}, bf16[8,512,3,64]{1,3,2,0:T(8,128)(2,1)}, bf16...) while((s32[]{:T(128)}, ...), condition=%wide.region_24.25_spmd, body=%wide.region_22.24_spmd.sunk | while | flops 511146496 | bytes 26125428 | solution.py:210
  598.8 11.7 fusion.140
  610.5 41.4 %reduce-scatter.12.cloned.1.call-done = bf16[1024,768]{0,1:T(8,128)(2,1)} async-done(((bf16[4096,768]{0,1:T(8,128)(2,1)}), bf16[1024,768]{0,1:T(8,128)(2,1)}) %reduce-scatter.12.cloned.1.call-update) | async-done | bytes 1572880 | tf_op jit(solution)/shard_map/reduce_scatter | solution.py:233
  659.1 18.5 %convert_reduce_fusion.1 = (f32[3072]{0:T(1024)S(1)}, bf16[1024,3072]{1,0:T(8,128)(2,1)}) fusion(f32[1024,3072]{1,0:T(8,128)} %get-tuple-element.437, bf16[1024,768]{0,1:T(8,128)(2,1)} %get-tuple-element.421, bf16[2,3072,768]{2,1,0:T(8,128)(2,1)} %param.33, f32[1024,3072]{1,0:T(8,128)} %get-tuple-element.479, f32[3072]{0:T(1024)S(1)} %bitcast.495), kind=kOutput, calls=%fused_computation.132 | convolution fusion | flops 4885312512 | bytes 37773312 | tf_op jit(solution)/shard_map/rd,fd->rf/dot_general | solution.py:185
  738.1 16.7 %pad_maximum_fusion = bf16[2,2,768,3072]{3,2,1,0:T(8,128)(2,1)} fusion(bf16[1,2,768,3072]{3,2,1,0:T(8,128)(2,1)} %maximum_bitcast_fusion.1, bf16[1,2,768,3072]{3,2,1,0:T(8,128)(2,1)} %maximum_bitcast_fusion), kind=kLoop, calls=%fused_computation.126 | loop fusion | flops 9437184 | bytes 37748736 | tf_op jit(solution)/shard_map/stack | solution.py:264
  802.2 101.9 %while.55 = (s32[]{:T(128)}, bf16[8,512,3,64]{1,3,2,0:T(8,128)(2,1)}, bf16[8,512,3,64]{1,3,2,0:T(8,128)(2,1)}, bf16[8,512,3,64]{1,3,2,0:T(8,128)(2,1)}, bf16[8,5...) while((s32[]{:T(128)}, ...), condition=%wide.region_32.33_spmd, body=%wide.region_30.32_spmd.sunk | while | flops 511146496 | bytes 26125428 | solution.py:210
  966.8 112.1 %reduce-scatter.18.cloned.1.call-done = bf16[2,2,96,3072]{3,2,1,0:T(8,128)(2,1)} async-done(((bf16[2,2,768,3072]{3,2,1,0:T(8,128)(2,1)}), bf16[2,2,96,3072]{3,2,1,0:T(8,128)(2,1)}) %reduce-scatter.18.cloned.1.call-update) | async-done | bytes 2359312 | tf_op jit(solution)/shard_map/reduce_scatter | solution.py:270
  1081.6 122.8 %all-reduce.3.cloned.1.call-done = (f32[2,8,768]{2,0,1:T(2,128)}, f32[2,3072]{1,0:T(2,128)}) async-done(((f32[2,8,768]{2,0,1:T(2,128)}, f32[2,3072]{1,0:T(2,128)}), (f32[2,8,768]{2,0,1:T(2,128)}, f32[2,3072]{1,0:T(2,128)})) %all-reduce.3.cloned.1.call-update) | async-done | bytes 73744 | tf_op jit(solution)/shard_map/psum | solution.py:288
  1207.1 69.8 %reduce-scatter.22.cloned.1.call-done = bf16[96,1152]{1,0:T(8,128)(2,1)} async-done(((bf16[768,1152]{1,0:T(8,128)(2,1)}), bf16[96,1152]{1,0:T(8,128)(2,1)}) %reduce-scatter.22.cloned.1.call-update) | async-done | bytes 221200
  1281.1 18.6 %reduce-scatter.24.cloned.1.call-done = bf16[192,192]{1,0:T(8,128)(2,1)} async-done(((bf16[768,192]{1,0:T(8,128)(2,1)}), bf16[192,192]{1,0:T(8,128)(2,1)}) %reduce-scatter.24.cloned.1.call-update) | async-done | bytes 73744
  1301.4 59.1 %reduce-scatter.14.cloned.1.call-done = bf16[1024,768]{0,1:T(8,128)(2,1)} async-done(((bf16[4096,768]{0,1:T(8,128)(2,1)}), bf16[1024,768]{0,1:T(8,128)(2,1)}) %reduce-scatter.14.cloned.1.call-update) | async-done | bytes 1572880 | tf_op jit(solution)/shard_map/reduce_scatter | solution.py:233
  1366.3 29.9 %reduce-scatter.20.cloned.1.call-done = bf16[2,2,96,768]{3,2,1,0:T(8,128)(2,1)} async-done(((bf16[2,2,96,3072]{3,2,1,0:T(8,128)(2,1)}), bf16[2,2,96,768]{3,2,1,0:T(8,128)(2,1)}) %reduce-scatter.20.cloned.1.call-update) | async-done | bytes 589840 | tf_op jit(solution)/shard_map/reduce_scatter | solution.py:281
  (599 shorter events, 623.1 us)
Async XLA Ops:
  7.2 51.5 %all-gather.3.cloned.1.call-start = ((), (), s32[]{:S(2)}) async-start(), calls=%async_computation.11 | async-start | bytes 7864320 | tf_op jit(solution)/shard_map/all_gather | solution.py:110
  130.6 23.8 %all-to-all-start = ((bf16[4,1024,192]{1,2,0:T(8,128)(2,1)}), bf16[4,1024,192]{1,2,0:T(8,128)(2,1)S(1)}, u32[]{:S(2)}, u32[]{:S(2)}) async-start(bf16[4,1024,192]{1,2,0:T(8,128)(2,1)} %copy.160), calls=%async_computation | async-start | bytes 3145728 | tf_op jit(solution)/shard_map/all_to_all | solution.py:127
  134.3 120.8 %all-gather.5.cloned.1.call-start = ((), (), s32[]{:S(2)}) async-start(), calls=%async_computation.12 | async-start | bytes 7864320 | tf_op jit(solution)/shard_map/all_gather | solution.py:110
  137.9 59.8 %copy-start.50 = (f32[768]{0:T(1024)}, f32[768]{0:T(1024)S(1)}, u32[]{:S(2)}) copy-start(f32[768]{0:T(1024)S(1)} %get-tuple-element.495) | copy-start | bytes 9220
  137.9 59.8 %copy-start.71 = (f32[768]{0:T(1024)}, f32[768]{0:T(1024)S(1)}, u32[]{:S(2)}) copy-start(f32[768]{0:T(1024)S(1)} %get-tuple-element.347) | copy-start | bytes 9220
  138.5 213.3 %copy-start.35 = (f32[768]{0:T(1024)}, f32[768]{0:T(1024)S(1)}, u32[]{:S(2)}) copy-start(f32[768]{0:T(1024)S(1)} %get-tuple-element.497) | copy-start | bytes 9220
  206.4 145.4 %copy-start = (f32[1024,768]{0,1:T(8,128)}, f32[1024,768]{0,1:T(8,128)S(1)}, u32[]{:S(2)}) copy-start(f32[1024,768]{0,1:T(8,128)S(1)} %get-tuple-element.481) | copy-start | bytes 9437188
  206.4 145.4 %copy-start.33 = (f32[1024]{0:T(1024)}, f32[1024]{0:T(1024)S(1)}, u32[]{:S(2)}) copy-start(f32[1024]{0:T(1024)S(1)} %broadcast_multiply_fusion.2) | copy-start | bytes 12292
  206.8 145.0 %copy-start.37 = (f32[1024]{0:T(1024)}, f32[1024]{0:T(1024)S(1)}, u32[]{:S(2)}) copy-start(f32[1024]{0:T(1024)S(1)} %fusion.190) | copy-start | bytes 12292
  327.0 24.8 %all-to-all-start.1 = ((bf16[4,1024,192]{1,2,0:T(8,128)(2,1)}), bf16[4,1024,192]{1,2,0:T(8,128)(2,1)}, u32[]{:S(2)}, u32[]{:S(2)}) async-start(bf16[4,1024,192]{1,2,0:T(8,128)(2,1)} %copy.166), calls=%async_computation.1 | async-start | bytes 3145728 | tf_op jit(solution)/shard_map/all_to_all | solution.py:127
  447.9 23.6 %all-to-all-start.2 = ((bf16[1024,4,192]{0,2,1:T(8,128)(2,1)}), bf16[1024,4,192]{0,2,1:T(8,128)(2,1)S(1)}, u32[]{:S(2)}, u32[]{:S(2)}) async-start(bf16[1024,4,192]{0,2,1:T(8,128)(2,1)} %bitcast.68), calls=%async_computation.2 | async-start | bytes 3145728 | tf_op jit(solution)/shard_map/all_to_all | solution.py:208
  451.4 200.5 %reduce-scatter.12.cloned.1.call-start = ((), (), s32[]{:S(2)}) async-start(), calls=%async_computation.13 | async-start | bytes 7864320 | tf_op jit(solution)/shard_map/reduce_scatter | solution.py:233
  593.4 361.3 %reduce-scatter.16.cloned.1.call-start = ((), (), s32[]{:S(2)}) async-start(), calls=%async_computation.15 | async-start | bytes 2654208 | tf_op jit(solution)/shard_map/reduce_scatter | solution.py:273
  598.8 53.1 %copy-start.1 = (f32[1024,768]{0,1:T(8,128)S(1)}, f32[1024,768]{0,1:T(8,128)}, u32[]{:S(2)}) copy-start(f32[1024,768]{0,1:T(8,128)} %copy-done) | copy-start | bytes 9437188
  598.8 53.1 %copy-start.34 = (f32[1024]{0:T(1024)S(1)}, f32[1024]{0:T(1024)}, u32[]{:S(2)}) copy-start(f32[1024]{0:T(1024)} %copy-done.33) | copy-start | bytes 12292
  598.8 53.1 %copy-start.36 = (f32[768]{0:T(1024)S(1)}, f32[768]{0:T(1024)}, u32[]{:S(2)}) copy-start(f32[768]{0:T(1024)} %copy-done.35) | copy-start | bytes 9220
  598.8 53.1 %copy-start.38 = (f32[1024]{0:T(1024)S(1)}, f32[1024]{0:T(1024)}, u32[]{:S(2)}) copy-start(f32[1024]{0:T(1024)} %copy-done.37) | copy-start | bytes 12292
  693.2 385.8 %reduce-scatter.18.cloned.1.call-start = ((), (), s32[]{:S(2)}) async-start(), calls=%async_computation.16 | async-start | bytes 21233664 | tf_op jit(solution)/shard_map/reduce_scatter | solution.py:270
  763.2 24.5 %all-to-all-start.3 = ((bf16[1024,4,192]{0,2,1:T(8,128)(2,1)}), bf16[1024,4,192]{0,2,1:T(8,128)(2,1)}, u32[]{:S(2)}, u32[]{:S(2)}) async-start(bf16[1024,4,192]{0,2,1:T(8,128)(2,1)} %bitcast.483), calls=%async_computation.4 | async-start | bytes 3145728 | tf_op jit(solution)/shard_map/all_to_all | solution.py:208
  767.6 436.8 %all-reduce.3.cloned.1.call-start = ((), (), s32[]{:S(2)}) async-start(), calls=%async_computation.20 | async-start | bytes 147456 | tf_op jit(solution)/shard_map/psum | solution.py:288
  932.0 344.8 %reduce-scatter.22.cloned.1.call-start = ((), (), s32[]{:S(2)}) async-start(), calls=%async_computation.18 | async-start | bytes 1990656
  954.6 345.0 %reduce-scatter.24.cloned.1.call-start = ((), (), s32[]{:S(2)}) async-start(), calls=%async_computation.19 | async-start | bytes 491520
  957.0 403.6 %reduce-scatter.14.cloned.1.call-start = ((), (), s32[]{:S(2)}) async-start(), calls=%async_computation.14 | async-start | bytes 7864320 | tf_op jit(solution)/shard_map/reduce_scatter | solution.py:233
  966.8 429.4 %reduce-scatter.20.cloned.1.call-start = ((), (), s32[]{:S(2)}) async-start(), calls=%async_computation.17 | async-start | bytes 2949120 | tf_op jit(solution)/shard_map/reduce_scatter | solution.py:281
  (75 other events, 1029.3 us)
Sparse Core Ops, SparseCore 0:
  9.6 49.0 all-gather.2
  208.7 46.3 all-gather.4
  593.5 58.3 reduce-scatter.11
  693.3 69.0 reduce-scatter.15
  766.6 312.3 reduce-scatter.17
  1086.6 117.7 all-reduce.2
  1208.2 68.5 reduce-scatter.21
  1279.9 19.7 reduce-scatter.23
  1302.2 58.3 reduce-scatter.13
  1363.1 33.0 reduce-scatter.19
where the time goes:
time: 1420 us; the launch traced here: 1410 us
  waiting for transfers between devices  610 us (43%)
  matrix products  475 us (33%)
  local copies, waits for them, and re-layouts  185 us (13%)
  other arithmetic  102 us (7%)
  starting transfers between devices  17.2 us (1%)
  between operations  15.7 us (1%)
    psum x1, waiting for transfers between devices, on_device(): small_sum, shift_sum = lax.psum((small_stack, shift_stack), ('dp', 'head'))  123 us
    reduce_scatter x1, waiting for transfers between devices, on_device(): lax.psum_scatter(ffn_stack.astype(jnp.bfloat16), 'dp', scatter_dimension=...  112 us
    reduce_scatter x2, waiting for transfers between devices, on_device(): lax.psum_scatter(jnp.einsum('rce,cde->rd', grad_proj, layer_weights, pref...  101 us
    all_gather x2, waiting for transfers between devices, on_device(): lax.all_gather(hidden_state.astype(jnp.bfloat16), 'head', axis=0, tiled=T...  92.3 us
    unnamed x12, waiting for transfers between devices  89.2 us
    dot_general x2, matrix products, on_device(): jnp.dot(ffn_rows, up_part, preferred_element_type=jnp.float32) + up_shift  77.2 us
    unnamed x195, local copies, waits for them, and re-layouts  57.6 us
    dot_general x32, matrix products, slot_scores(): jnp.einsum('qhd,khd->hqk', queries, keys_in, preferred_element_type=jnp.f...  55.1 us
  transfers between devices with their start and end apart: 14, of which 13 were waited for; matrix products, arithmetic and copies ran while one was open for 21% of the time, Pallas kernels for 0%

commit v1 on v0

--- a/solution.py
+++ b/solution.py
@@ -2,6 +2,7 @@
 import jax.numpy as jnp
 from jax import lax
 from jax.sharding import PartitionSpec as P
+from jax.lax import psum
 
 HD = 64
 EPSILON = 1e-06
@@ -285,7 +286,8 @@
             proj_data.astype(jnp.bfloat16), "head", scatter_dimension=2, tiled=True
         ).astype(jnp.float32),
     )
-    small_sum, shift_sum = lax.psum((small_stack, shift_stack), ("dp", "head"))
+    spot_draft = lambda u, peer_axis, chip_axis: psum(psum(u, peer_axis), chip_axis)
+    small_sum, shift_sum = spot_draft((small_stack, shift_stack), "head", "dp")
     down_weight_grad = jnp.transpose(ffn_head[:, 1], (0, 2, 1))
     return (
         out_state,

time: 1420 us -> 1570 us (1.11)
  waiting for transfers between devices: 610 us -> 751 us
    reduce_scatter x1, waiting for transfers between devices: 112 us -> 304 us  [on_device(): lax.psum_scatter(ffn_stack.astype(jnp.bfloat16), 'dp', scatter_dimension=...]
    psum x1 -> x2, waiting for transfers between devices: 123 us -> 68.9 us  [the longest x1 68.9 us: on_device(): psum(psum(u, peer_axis), chip_axis)]
    unnamed x12 -> x13, waiting for transfers between devices: 89.2 us -> 86.2 us
    unnamed x195 -> x175, local copies, waits for them, and re-layouts: 57.6 us -> 59.4 us
  transfers between devices with their start and end apart: 14 -> 15, of which waited for: 13 -> 14; matrix products, arithmetic and copies ran while one was open for 21% -> 11% of each run, Pallas kernels for 0% -> 0%
where the time goes in v1:
time: 1570 us; the launch traced here: 1550 us
  waiting for transfers between devices  751 us (48%)
  matrix products  475 us (30%)
  local copies, waits for them, and re-layouts  187 us (12%)
  other arithmetic  106 us (7%)
  starting transfers between devices  17.3 us (1%)
    reduce_scatter x1, waiting for transfers between devices, on_device(): lax.psum_scatter(ffn_stack.astype(jnp.bfloat16), 'dp', scatter_dimension=...  304 us
    reduce_scatter x2, waiting for transfers between devices, on_device(): lax.psum_scatter(jnp.einsum('rce,cde->rd', grad_proj, layer_weights, pref...  101 us
    all_gather x2, waiting for transfers between devices, on_device(): lax.all_gather(hidden_state.astype(jnp.bfloat16), 'head', axis=0, tiled=T...  92.3 us
    unnamed x13, waiting for transfers between devices  86.2 us
    dot_general x2, matrix products, on_device(): jnp.dot(ffn_rows, up_part, preferred_element_type=jnp.float32) + up_shift  77.2 us
    psum x1, waiting for transfers between devices, on_device(): psum(psum(u, peer_axis), chip_axis)  68.9 us
    unnamed x175, local copies, waits for them, and re-layouts  59.4 us
    dot_general x32, matrix products, slot_scores(): jnp.einsum('qhd,khd->hqk', queries, keys_in, preferred_element_type=jnp.f...  55 us
  transfers between devices with their start and end apart: 15, of which 14 were waited for; matrix products, arithmetic and copies ran while one was open for 11% of the time, Pallas kernels for 0%

profile of v1, /device:TPU:0, one launch (start us, length us, event | category | flops | bytes accessed | tf_op | source)
XLA Modules:
  0.0 1552.8 jit_solution(5373393553655973951)
XLA Ops:
  12.9 45.8 %all-gather.3.cloned.1.call-done = bf16[4096,768]{1,0:T(8,128)(2,1)} async-done(((bf16[1024,768]{1,0:T(8,128)(2,1)}), bf16[4096,768]{1,0:T(8,128)(2,1)}) %all-gather.3.cloned.1.call-update) | async-done | bytes 6291472 | tf_op jit(solution)/shard_map/all_gather | solution.py:111
  73.9 35.4 %while.52 = (s32[]{:T(128)}, bf16[8,512,3,64]{1,3,2,0:T(8,128)(2,1)}, f32[8,3,512]{2,1,0:T(4,128)S(1)}, bf16[8,512,3,64]{1,3,2,0:T(8,128)(2,1)}, s32[8,512]{1,0:...) while((s32[]{:T(128)}, ...), condition=%wide.region_5.6_spmd, body=%wide.region_2.5_spmd.sunk | while | flops 211122688 | bytes 11335773 | solution.py:124
  113.8 13.7 all_to_all.52
  139.1 15.2 all-to-all-done
  158.9 38.8 %multiply_convert_fusion.3 = (bf16[1024,3072]{1,0:T(8,128)(2,1)}, f32[1024,3072]{1,0:T(8,128)}, f32[1024,3072]{1,0:T(8,128)}) fusion(f32[3072]{0:T(1024)S(1)} %bitcast.494, bf16[2,768,3072]{2,1,0:T(8,128)(2,1)} %param.31, f32[1024,768]{0,1:T(8,128)S(1)} %get-tuple-element.480, f32[768]{0:T(1024)S(1)} %get-tuple-element.347, ...), kind=kOutput, calls=%fused_computation.148 | convolution fusion | flops 5043388416 | bytes 39348224 | tf_op jit(solution)/shard_map/dot_general | solution.py:140
  208.6 46.5 %all-gather.5.cloned.1.call-done = bf16[4096,768]{0,1:T(8,128)(2,1)} async-done(((bf16[1024,768]{0,1:T(8,128)(2,1)}), bf16[4096,768]{0,1:T(8,128)(2,1)}) %all-gather.5.cloned.1.call-update) | async-done | bytes 6291472 | tf_op jit(solution)/shard_map/all_gather | solution.py:111
  273.2 43.5 %while.53 = (s32[]{:T(128)}, bf16[8,512,3,64]{1,3,2,0:T(8,128)(2,1)}, f32[8,3,512]{2,1,0:T(4,128)S(1)}, bf16[8,512,3,64]{1,3,2,0:T(8,128)(2,1)}, s32[8,512]{1,0:...) while((s32[]{:T(128)}, ...), condition=%wide.region_13.14_spmd, body=%wide.region_10.13_spmd.sunk | while | flops 211122688 | bytes 11335773 | solution.py:124
  334.2 17.5 %all-to-all-done.1 = bf16[4,1024,192]{1,2,0:T(8,128)(2,1)} async-done(((bf16[4,1024,192]{1,2,0:T(8,128)(2,1)}), bf16[4,1024,192]{1,2,0:T(8,128)(2,1)}, u32[]{:S(2)}, u32[]{:S(2)}) %all-to-all-start.1) | async-done | bytes 1572896 | tf_op jit(solution)/shard_map/all_to_all | solution.py:128
  356.4 38.4 %multiply_convert_fusion.2 = (bf16[1024,3072]{1,0:T(8,128)(2,1)}, f32[1024,3072]{1,0:T(8,128)}, f32[1024,3072]{1,0:T(8,128)}) fusion(f32[3072]{0:T(1024)S(1)} %bitcast.497, bf16[2,768,3072]{2,1,0:T(8,128)(2,1)} %param.31, f32[1024,768]{0,1:T(8,128)S(1)} %get-tuple-element.485, f32[768]{0:T(1024)S(1)} %copy-done.64, f32[768]{0:T(1024)S(1)} %copy-done.48, ...), kind=kOutput, calls=%fused_computation.135 | convolution fusion | flops 5043388416 | bytes 39348224 | tf_op jit(solution)/shard_map/dot_general | solution.py:140
  409.3 17.6 %convert_reduce_fusion = (f32[3072]{0:T(1024)S(1)}, bf16[1024,3072]{1,0:T(8,128)(2,1)}) fusion(f32[1024,3072]{1,0:T(8,128)} %get-tuple-element.437, bf16[1024,768]{0,1:T(8,128)(2,1)S(1)} %get-tuple-element.427, bf16[2,3072,768]{2,1,0:T(8,128)(2,1)} %param.33, f32[1024,3072]{1,0:T(8,128)} %get-tuple-element.486, f32[3072]{0:T(1024)S(1)} %bitcast.498), kind=kOutput, calls=%fused_computation.131 | convolution fusion | flops 4885312512 | bytes 37773312 | tf_op jit(solution)/shard_map/rd,fd->rf/dot_general | solution.py:186
  448.5 20.0 %all-to-all-done.2 = bf16[1024,4,192]{0,2,1:T(8,128)(2,1)S(1)} async-done(((bf16[1024,4,192]{0,2,1:T(8,128)(2,1)}), bf16[1024,4,192]{0,2,1:T(8,128)(2,1)S(1)}, u32[]{:S(2)}, u32[]{:S(2)}) %all-to-all-start.2) | async-done | bytes 1572896 | tf_op jit(solution)/shard_map/all_to_all | solution.py:209
  476.6 88.1 %while.54 = (s32[]{:T(128)}, bf16[8,512,3,64]{1,3,2,0:T(8,128)(2,1)S(1)}, bf16[8,512,3,64]{1,3,2,0:T(8,128)(2,1)}, bf16[8,512,3,64]{1,3,2,0:T(8,128)(2,1)}, bf16...) while((s32[]{:T(128)}, ...), condition=%wide.region_24.25_spmd, body=%wide.region_22.24_spmd.sunk | while | flops 511146496 | bytes 26125428 | solution.py:211
  596.0 11.7 fusion.140
  607.7 41.4 %reduce-scatter.12.cloned.1.call-done = bf16[1024,768]{0,1:T(8,128)(2,1)} async-done(((bf16[4096,768]{0,1:T(8,128)(2,1)}), bf16[1024,768]{0,1:T(8,128)(2,1)}) %reduce-scatter.12.cloned.1.call-update) | async-done | bytes 1572880 | tf_op jit(solution)/shard_map/reduce_scatter | solution.py:234
  656.5 18.5 %convert_reduce_fusion.1 = (f32[3072]{0:T(1024)S(1)}, bf16[1024,3072]{1,0:T(8,128)(2,1)}) fusion(f32[1024,3072]{1,0:T(8,128)} %get-tuple-element.439, bf16[1024,768]{0,1:T(8,128)(2,1)} %get-tuple-element.423, bf16[2,3072,768]{2,1,0:T(8,128)(2,1)} %param.33, f32[1024,3072]{1,0:T(8,128)} %get-tuple-element.481, f32[3072]{0:T(1024)S(1)} %bitcast.495), kind=kOutput, calls=%fused_computation.132 | convolution fusion | flops 4885312512 | bytes 37773312 | tf_op jit(solution)/shard_map/rd,fd->rf/dot_general | solution.py:186
  703.5 11.6 all-to-all-done.3
  729.4 101.6 %while.55 = (s32[]{:T(128)}, bf16[8,512,3,64]{1,3,2,0:T(8,128)(2,1)}, bf16[8,512,3,64]{1,3,2,0:T(8,128)(2,1)}, bf16[8,512,3,64]{1,3,2,0:T(8,128)(2,1)}, bf16[8,5...) while((s32[]{:T(128)}, ...), condition=%wide.region_32.33_spmd, body=%wide.region_30.32_spmd.sunk | while | flops 511146496 | bytes 26125428 | solution.py:211
  910.6 16.7 %pad_maximum_fusion = bf16[2,2,768,3072]{3,2,1,0:T(8,128)(2,1)} fusion(bf16[1,2,768,3072]{3,2,1,0:T(8,128)(2,1)} %maximum_bitcast_fusion.1, bf16[1,2,768,3072]{3,2,1,0:T(8,128)(2,1)} %maximum_bitcast_fusion), kind=kLoop, calls=%fused_computation.126 | loop fusion | flops 9437184 | bytes 37748736 | tf_op jit(solution)/shard_map/stack | solution.py:265
  978.5 304.0 %reduce-scatter.18.cloned.1.call-done = bf16[2,2,96,3072]{3,2,1,0:T(8,128)(2,1)} async-done(((bf16[2,2,768,3072]{3,2,1,0:T(8,128)(2,1)}), bf16[2,2,96,3072]{3,2,1,0:T(8,128)(2,1)}) %reduce-scatter.18.cloned.1.call-update) | async-done | bytes 2359312 | tf_op jit(solution)/shard_map/reduce_scatter | solution.py:271
  1285.1 68.9 %all-reduce.5.cloned.1.call-done = (f32[2,8,768]{2,0,1:T(2,128)}, f32[2,3072]{1,0:T(2,128)}) async-done(((f32[2,8,768]{2,0,1:T(2,128)}, f32[2,3072]{1,0:T(2,128)}), (f32[2,8,768]{2,0,1:T(2,128)}, f32[2,3072]{1,0:T(2,128)})) %all-reduce.5.cloned.1.call-update) | async-done | bytes 73744 | tf_op jit(solution)/shard_map/psum | solution.py:289
  1356.7 66.7 %reduce-scatter.22.cloned.1.call-done = bf16[96,1152]{1,0:T(8,128)(2,1)} async-done(((bf16[768,1152]{1,0:T(8,128)(2,1)}), bf16[96,1152]{1,0:T(8,128)(2,1)}) %reduce-scatter.22.cloned.1.call-update) | async-done | bytes 221200
  1427.6 18.7 %reduce-scatter.24.cloned.1.call-done = bf16[192,192]{1,0:T(8,128)(2,1)} async-done(((bf16[768,192]{1,0:T(8,128)(2,1)}), bf16[192,192]{1,0:T(8,128)(2,1)}) %reduce-scatter.24.cloned.1.call-update) | async-done | bytes 73744
  1448.1 59.1 %reduce-scatter.14.cloned.1.call-done = bf16[1024,768]{0,1:T(8,128)(2,1)} async-done(((bf16[4096,768]{0,1:T(8,128)(2,1)}), bf16[1024,768]{0,1:T(8,128)(2,1)}) %reduce-scatter.14.cloned.1.call-update) | async-done | bytes 1572880 | tf_op jit(solution)/shard_map/reduce_scatter | solution.py:234
  1513.0 29.9 %reduce-scatter.20.cloned.1.call-done = bf16[2,2,96,768]{3,2,1,0:T(8,128)(2,1)} async-done(((bf16[2,2,96,3072]{3,2,1,0:T(8,128)(2,1)}), bf16[2,2,96,768]{3,2,1,0:T(8,128)(2,1)}) %reduce-scatter.20.cloned.1.call-update) | async-done | bytes 589840 | tf_op jit(solution)/shard_map/reduce_scatter | solution.py:282
  (582 shorter events, 635.5 us)
Async XLA Ops:
  7.2 51.5 %all-gather.3.cloned.1.call-start = ((), (), s32[]{:S(2)}) async-start(), calls=%async_computation.11 | async-start | bytes 7864320 | tf_op jit(solution)/shard_map/all_gather | solution.py:111
  130.6 23.8 %all-to-all-start = ((bf16[4,1024,192]{1,2,0:T(8,128)(2,1)}), bf16[4,1024,192]{1,2,0:T(8,128)(2,1)S(1)}, u32[]{:S(2)}, u32[]{:S(2)}) async-start(bf16[4,1024,192]{1,2,0:T(8,128)(2,1)} %copy.160), calls=%async_computation | async-start | bytes 3145728 | tf_op jit(solution)/shard_map/all_to_all | solution.py:128
  134.3 120.8 %all-gather.5.cloned.1.call-start = ((), (), s32[]{:S(2)}) async-start(), calls=%async_computation.12 | async-start | bytes 7864320 | tf_op jit(solution)/shard_map/all_gather | solution.py:111
  137.9 59.8 %copy-start.46 = (f32[768]{0:T(1024)}, f32[768]{0:T(1024)S(1)}, u32[]{:S(2)}) copy-start(f32[768]{0:T(1024)S(1)} %get-tuple-element.497) | copy-start | bytes 9220
  137.9 59.8 %copy-start.62 = (f32[768]{0:T(1024)}, f32[768]{0:T(1024)S(1)}, u32[]{:S(2)}) copy-start(f32[768]{0:T(1024)S(1)} %get-tuple-element.347) | copy-start | bytes 9220
  138.5 213.2 %copy-start.31 = (f32[768]{0:T(1024)}, f32[768]{0:T(1024)S(1)}, u32[]{:S(2)}) copy-start(f32[768]{0:T(1024)S(1)} %get-tuple-element.499) | copy-start | bytes 9220
  206.4 145.3 %copy-start = (f32[1024,768]{0,1:T(8,128)}, f32[1024,768]{0,1:T(8,128)S(1)}, u32[]{:S(2)}) copy-start(f32[1024,768]{0,1:T(8,128)S(1)} %get-tuple-element.483) | copy-start | bytes 9437188
  206.4 145.3 %copy-start.29 = (f32[1024]{0:T(1024)}, f32[1024]{0:T(1024)S(1)}, u32[]{:S(2)}) copy-start(f32[1024]{0:T(1024)S(1)} %broadcast_multiply_fusion.2) | copy-start | bytes 12292
  206.8 144.9 %copy-start.33 = (f32[1024]{0:T(1024)}, f32[1024]{0:T(1024)S(1)}, u32[]{:S(2)}) copy-start(f32[1024]{0:T(1024)S(1)} %fusion.190) | copy-start | bytes 12292
  327.0 24.8 %all-to-all-start.1 = ((bf16[4,1024,192]{1,2,0:T(8,128)(2,1)}), bf16[4,1024,192]{1,2,0:T(8,128)(2,1)}, u32[]{:S(2)}, u32[]{:S(2)}) async-start(bf16[4,1024,192]{1,2,0:T(8,128)(2,1)} %copy.166), calls=%async_computation.1 | async-start | bytes 3145728 | tf_op jit(solution)/shard_map/all_to_all | solution.py:128
  444.9 23.6 %all-to-all-start.2 = ((bf16[1024,4,192]{0,2,1:T(8,128)(2,1)}), bf16[1024,4,192]{0,2,1:T(8,128)(2,1)S(1)}, u32[]{:S(2)}, u32[]{:S(2)}) async-start(bf16[1024,4,192]{0,2,1:T(8,128)(2,1)} %bitcast.68), calls=%async_computation.2 | async-start | bytes 3145728 | tf_op jit(solution)/shard_map/all_to_all | solution.py:209
  448.5 200.6 %reduce-scatter.12.cloned.1.call-start = ((), (), s32[]{:S(2)}) async-start(), calls=%async_computation.13 | async-start | bytes 7864320 | tf_op jit(solution)/shard_map/reduce_scatter | solution.py:234
  596.0 53.1 %copy-start.1 = (f32[1024,768]{0,1:T(8,128)S(1)}, f32[1024,768]{0,1:T(8,128)}, u32[]{:S(2)}) copy-start(f32[1024,768]{0,1:T(8,128)} %copy-done) | copy-start | bytes 9437188
  596.0 53.1 %copy-start.30 = (f32[1024]{0:T(1024)S(1)}, f32[1024]{0:T(1024)}, u32[]{:S(2)}) copy-start(f32[1024]{0:T(1024)} %copy-done.29) | copy-start | bytes 12292
  596.0 53.1 %copy-start.32 = (f32[768]{0:T(1024)S(1)}, f32[768]{0:T(1024)}, u32[]{:S(2)}) copy-start(f32[768]{0:T(1024)} %copy-done.31) | copy-start | bytes 9220
  690.5 24.5 %all-to-all-start.3 = ((bf16[1024,4,192]{0,2,1:T(8,128)(2,1)}), bf16[1024,4,192]{0,2,1:T(8,128)(2,1)}, u32[]{:S(2)}, u32[]{:S(2)}) async-start(bf16[1024,4,192]{0,2,1:T(8,128)(2,1)} %bitcast.483), calls=%async_computation.4 | async-start | bytes 3145728 | tf_op jit(solution)/shard_map/all_to_all | solution.py:209
  694.9 251.0 %all-reduce.7.cloned.1.call-start = ((), (), s32[]{:S(2)}) async-start(), calls=%async_computation.21 | async-start | bytes 147456 | tf_op jit(solution)/shard_map/psum | solution.py:289
  862.3 104.1 %reduce-scatter.16.cloned.1.call-start = ((), (), s32[]{:S(2)}) async-start(), calls=%async_computation.15 | async-start | bytes 2654208 | tf_op jit(solution)/shard_map/reduce_scatter | solution.py:274
  865.6 416.9 %reduce-scatter.18.cloned.1.call-start = ((), (), s32[]{:S(2)}) async-start(), calls=%async_computation.16 | async-start | bytes 21233664 | tf_op jit(solution)/shard_map/reduce_scatter | solution.py:271
  927.4 426.6 %all-reduce.5.cloned.1.call-start = ((), (), s32[]{:S(2)}) async-start(), calls=%async_computation.20 | async-start | bytes 147456 | tf_op jit(solution)/shard_map/psum | solution.py:289
  945.9 477.5 %reduce-scatter.22.cloned.1.call-start = ((), (), s32[]{:S(2)}) async-start(), calls=%async_computation.18 | async-start | bytes 1990656
  961.7 484.7 %reduce-scatter.24.cloned.1.call-start = ((), (), s32[]{:S(2)}) async-start(), calls=%async_computation.19 | async-start | bytes 491520
  968.6 538.6 %reduce-scatter.14.cloned.1.call-start = ((), (), s32[]{:S(2)}) async-start(), calls=%async_computation.14 | async-start | bytes 7864320 | tf_op jit(solution)/shard_map/reduce_scatter | solution.py:234
  978.2 564.7 %reduce-scatter.20.cloned.1.call-start = ((), (), s32[]{:S(2)}) async-start(), calls=%async_computation.17 | async-start | bytes 2949120 | tf_op jit(solution)/shard_map/reduce_scatter | solution.py:282
  (66 other events, 1059.3 us)
Sparse Core Ops, SparseCore 0:
  9.6 49.0 all-gather.2
  208.7 46.3 all-gather.4
  590.7 58.3 reduce-scatter.11
  862.4 29.4 all-reduce.6
  895.3 71.0 reduce-scatter.15
  970.1 312.3 reduce-scatter.17
  1286.1 67.8 all-reduce.4
  1357.5 65.8 reduce-scatter.21
  1426.6 19.6 reduce-scatter.23
  1448.9 58.3 reduce-scatter.13
  1509.8 33.0 reduce-scatter.19
